TPU v7x, 32 devices: a whole 2x2x4 slice. The times are simulated.
32 devices in a mesh: rep: 8 (over y, x, core), tp: 4 (over z).
Axes of the slice: x: 2, y: 2, z: 4, core: 2. Of those that a mesh axis runs over, the one named last changes fastest.
Arguments:
- hidden: bfloat16 [512, 8192], P('rep'), may hold values from -6 to 6
- norm_gain: bfloat16 [8192], replicated, may hold values from 0.5 to 1.5
- query_weight_matrix: bfloat16 [8192, 4096], P(None, 'tp'), may hold values from -0.0625 to 0.0625
- key_value_weight: bfloat16 [2, 8192, 1024], P(None, None, 'tp'), may hold values from -0.0625 to 0.0625
- output_weight_matrix: bfloat16 [4096, 8192], P('tp'), may hold values from -0.375 to 0.375
- input_down_factors: bfloat16 [3, 8192, 64], P(None, ('rep', 'tp')), may hold values from -0.0625 to 0.0625
- query_up_factor: bfloat16 [64, 4096], P(None, ('rep', 'tp')), may hold values from -0.75 to 0.75
- key_value_up_factors: bfloat16 [2, 64, 1024], P(None, None, ('rep', 'tp')), may hold values from -0.75 to 0.75
- output_down_factor: bfloat16 [4096, 64], P(('rep', 'tp')), may hold values from -0.375 to 0.375
- output_up_factor: bfloat16 [64, 8192], P(None, ('rep', 'tp')), may hold values from -0.75 to 0.75
- cache_keys: bfloat16 [512, 8, 128, 128], P('rep', 'tp'), may hold values from -360 to 360
- cache_values: bfloat16 [512, 8, 128, 128], P('rep', 'tp'), may hold values from -6 to 6
- lengths: int32 [512], P('rep'), may hold values from 1 to 127
Outputs:
- attn_out: bfloat16 [512, 8192], P('rep', 'tp')
All inputs are finite; a program needn't handle non-finite values.
Results may differ from a plain program's by a relative error of at most 0.03.
Values may be sent and summed in bfloat16 or wider, within the bound.
A program may use at most 128 MiB of HBM per device.

v0:
```python
import math

import jax
import jax.numpy as jnp
from jax import lax
from jax.sharding import PartitionSpec as P

epsilon = 1e-06
rope_base = 1000000.0
adapter_scale = 0.5


def rope_angles(lengths, head_dim):
    half_dim = head_dim // 2
    frequency = rope_base ** (-(jnp.arange(half_dim, dtype=jnp.float32) * 2.0) / head_dim)
    return lengths.astype(jnp.float32)[:, None] * frequency[None, :]


def rotate(vectors, angles):
    half_dim = vectors.shape[-1] // 2
    cosine = jnp.cos(angles)[:, None, :]
    sine_part = jnp.sin(angles)[:, None, :]
    low_half = vectors[..., :half_dim]
    high_half = vectors[..., half_dim:]
    return jnp.concatenate(
        [low_half * cosine - high_half * sine_part, high_half * cosine + low_half * sine_part],
        axis=-1,
    )


def adapted(normed, frozen_matrix, inner_part, up_factor):
    base_part = jnp.dot(normed, frozen_matrix, preferred_element_type=jnp.float32)
    return base_part + adapter_scale * jnp.dot(
        inner_part, up_factor, preferred_element_type=jnp.float32
    )


def attend(query, new_key, new_value, keys, values, lengths):
    score_scale = 1.0 / math.sqrt(keys.shape[-1])
    scores = (
        jnp.einsum(
            "bkgd,bkld->bkgl", query, keys.astype(jnp.float32), precision=lax.Precision.HIGHEST
        )
        * score_scale
    )
    own_score = jnp.sum(query * new_key.astype(jnp.float32)[:, :, None, :], axis=-1) * score_scale
    live_mask = (
        jnp.arange(keys.shape[2], dtype=jnp.int32)[None, None, None, :]
        < lengths[:, None, None, None]
    )
    row_max = jnp.maximum(jnp.max(jnp.where(live_mask, scores, -1e30), axis=-1), own_score)
    weights = jnp.where(live_mask, jnp.exp(scores - row_max[..., None]), 0.0)
    own_weight = jnp.exp(own_score - row_max)
    denom_sum = jnp.sum(weights, axis=-1) + own_weight
    probs = (weights / denom_sum[..., None]).astype(jnp.bfloat16)
    own_prob = (own_weight / denom_sum).astype(jnp.bfloat16)
    context = jnp.einsum("bkgl,bkld->bkgd", probs, values, preferred_element_type=jnp.float32)
    context = (
        context
        + own_prob.astype(jnp.float32)[..., None] * new_value.astype(jnp.float32)[:, :, None, :]
    )
    return context.astype(jnp.bfloat16)


def regroup(factor, tp_count, group):
    count, rank_dim, wide = factor.shape
    return factor.reshape(count, rank_dim, tp_count, group, wide // (tp_count * group))


def settle(factor):
    count, rank_dim, tp_count, group, piece = factor.shape
    return jnp.swapaxes(factor, 2, 3).reshape(count, rank_dim, group * tp_count * piece)


def local(
    hidden,
    norm_gain,
    query_weight_matrix,
    key_value_weight,
    output_weight_matrix,
    input_down_factors,
    query_up_factor,
    key_value_up_factors,
    output_down_factor,
    output_up_factor,
    cache_keys,
    cache_values,
    lengths,
):
    states = hidden.astype(jnp.float32)
    square = jnp.mean(states * states, axis=-1, keepdims=True)
    normed = (states * lax.rsqrt(square + epsilon) * norm_gain.astype(jnp.float32)).astype(
        jnp.bfloat16
    )
    seq_count = hidden.shape[0]
    block_rows = input_down_factors.shape[1]
    rep_count = lax.axis_size("rep")
    tp_count = lax.axis_size("tp")
    tp_index = lax.axis_index("tp")
    own_features = lax.dynamic_slice_in_dim(
        normed.reshape(seq_count, rep_count, tp_count, block_rows), tp_index, 1, 2
    )
    own_features = own_features.reshape(seq_count, rep_count * block_rows)
    partial_inner = jnp.einsum(
        "bd,jdr->jbr",
        own_features,
        lax.all_gather(input_down_factors, "rep", axis=1, tiled=True),
        preferred_element_type=jnp.float32,
    )
    inner = lax.psum(partial_inner.astype(jnp.bfloat16), "tp")
    query_up_rows = query_up_factor[None]
    out_down_rows = jnp.swapaxes(output_down_factor, 0, 1)[None]
    out_up_rows = output_up_factor[None]
    per_rep = (
        lax.all_gather(query_up_rows, "rep", axis=2, tiled=True),
        lax.all_gather(key_value_up_factors, "rep", axis=2, tiled=True),
        lax.all_gather(out_down_rows, "rep", axis=2, tiled=True),
        lax.all_gather(out_up_rows, "rep", axis=2, tiled=True),
    )
    group = rep_count // tp_count
    arrived = (
        lax.all_to_all(
            regroup(per_rep[0], tp_count, group), "tp", split_axis=2, concat_axis=2, tiled=True
        ),
        lax.all_to_all(
            regroup(per_rep[1], tp_count, group), "tp", split_axis=2, concat_axis=2, tiled=True
        ),
        lax.all_to_all(
            regroup(per_rep[2], tp_count, group), "tp", split_axis=2, concat_axis=2, tiled=True
        ),
        lax.all_to_all(
            regroup(per_rep[3], tp_count, group), "tp", split_axis=2, concat_axis=2, tiled=True
        ),
    )
    query_up_local = settle(arrived[0])
    key_value_up_local = settle(arrived[1])
    out_down_local = settle(arrived[2])
    out_up_local = settle(arrived[3])
    kv_local = cache_keys.shape[1]
    head_dim = cache_keys.shape[3]
    angles = rope_angles(lengths, head_dim)
    query = adapted(normed, query_weight_matrix, inner[0], query_up_local[0]).reshape(
        seq_count, -1, head_dim
    )
    query = rotate(query, angles).reshape(seq_count, kv_local, -1, head_dim)
    new_key = adapted(normed, key_value_weight[0], inner[1], key_value_up_local[0]).reshape(
        seq_count, kv_local, head_dim
    )
    new_key = rotate(new_key, angles).astype(jnp.bfloat16)
    new_value = (
        adapted(normed, key_value_weight[1], inner[2], key_value_up_local[1])
        .reshape(seq_count, kv_local, head_dim)
        .astype(jnp.bfloat16)
    )
    context = attend(query, new_key, new_value, cache_keys, cache_values, lengths).reshape(
        seq_count, -1
    )
    partial_middle = jnp.einsum(
        "bh,rh->br", context, out_down_local[0], preferred_element_type=jnp.float32
    )
    middle = lax.psum(partial_middle, "tp").astype(jnp.bfloat16)
    partial_value = jnp.dot(context, output_weight_matrix, preferred_element_type=jnp.float32)
    summed = lax.psum_scatter(
        partial_value.astype(jnp.bfloat16), "tp", scatter_dimension=1, tiled=True
    ).astype(jnp.float32)
    summed = summed + adapter_scale * jnp.dot(
        middle, out_up_local[0], preferred_element_type=jnp.float32
    )
    return summed.astype(jnp.bfloat16)


def solution(mesh):
    return jax.shard_map(
        local,
        mesh=mesh,
        in_specs=(
            P("rep", None),
            P(),
            P(None, "tp"),
            P(None, None, "tp"),
            P("tp", None),
            P(None, ("rep", "tp"), None),
            P(None, ("rep", "tp")),
            P(None, None, ("rep", "tp")),
            P(("rep", "tp"), None),
            P(None, ("rep", "tp")),
            P("rep", "tp", None, None),
            P("rep", "tp", None, None),
            P("rep"),
        ),
        out_specs=P("rep", "tp"),
        check_vma=False,
    )
```

profile of v0, /device:TPU:0, one launch (start us, length us, event | category | flops | bytes accessed | tf_op | source)
XLA Modules:
  0.0 177.4 jit_solution(7634904349694602952)
XLA Ops:
  6.5 10.9 %all_gather.17 = bf16[2,64,256]{1,2,0:T(8,128)(2,1)S(1)} all-gather(bf16[2,64,32]{1,2,0:T(8,128)(2,1)} %param.20), channel_id=1, replica_groups=mesh['rep'=8,'tp'=4] {'rep'}, dimensions={2}, use_global_device_ids=true | all-gather | bytes 73728 | tf_op jit(solution)/shard_map/all_gather | solution.py:116
  17.4 0.8 reshape.203
  18.2 4.9 %all-to-all-start.1 = ((bf16[4,2,4096]{2,1,0:T(2,128)(2,1)}), bf16[4,2,4096]{2,1,0:T(2,128)(2,1)S(1)}, u32[]{:S(2)}, u32[]{:S(2)}) async-start(bf16[4,2,4096]{2,1,0:T(2,128)(2,1)} %reshape.203), calls=%async_computation.1 | async-start | bytes 131072 | tf_op jit(solution)/shard_map/all_to_all | solution.py:125
  23.1 0.7 convert_element_type.82
  23.8 1.5 fusion.8
  25.4 1.5 fusion.10
  26.9 0.8 reshape.182
  27.7 3.0 %fusion.2 = f32[64,256]{1,0:T(8,128)S(1)} fusion(bf16[64,8192]{1,0:T(8,128)(2,1)S(1)} %fusion.10, bf16[2,8192,256]{2,1,0:T(8,128)(2,1)} %param.16), kind=kOutput, calls=%fused_computation.3 | convolution fusion | flops 268435456 | bytes 5308416 | tf_op jit(solution)/shard_map/dot_general | solution.py:32
  30.7 0.0 copy-start.2
  30.7 3.0 %fusion = f32[64,256]{1,0:T(8,128)S(1)} fusion(bf16[64,8192]{1,0:T(8,128)(2,1)S(1)} %fusion.10, bf16[2,8192,256]{2,1,0:T(8,128)(2,1)} %param.16), kind=kOutput, calls=%fused_computation.1 | convolution fusion | flops 268435456 | bytes 5308416 | tf_op jit(solution)/shard_map/dot_general | solution.py:32
  33.8 1.5 dynamic-slice_reduce_fusion
  35.3 0.1 reshape.199
  35.5 12.6 %all_gather.15 = bf16[3,2048,64]{1,2,0:T(8,128)(2,1)S(1)} all-gather(bf16[3,256,64]{1,2,0:T(8,128)(2,1)S(1)} %copy-done), channel_id=1, replica_groups=mesh['rep'=8,'tp'=4] {'rep'}, dimensions={1}, use_global_device_ids=true | all-gather | bytes 884736 | tf_op jit(solution)/shard_map/all_gather | solution.py:107
  48.0 0.4 fusion.17
  48.5 0.2 multiply_cosine_fusion
  48.7 0.1 iota_compare_fusion
  48.8 8.3 %all-gather = bf16[64,1024]{1,0:T(8,128)(2,1)S(1)} all-gather(bf16[64,128]{1,0:T(8,128)(2,1)S(1)} %copy-done.2), channel_id=2, replica_groups=mesh['rep'=8,'tp'=4] {'rep'}, dimensions={1}, use_global_device_ids=true | all-gather | bytes 147456 | tf_op jit(solution)/shard_map/all_gather | solution.py:115
  57.0 0.1 reshape.184
  57.1 0.7 copy.50
  57.9 19.8 %psum.14 = bf16[3,64,64]{2,1,0:T(8,128)(2,1)S(1)} all-reduce(bf16[3,64,64]{2,1,0:T(8,128)(2,1)S(1)} %fusion.17), channel_id=1, replica_groups=mesh['rep'=8,'tp'=4] {'tp'}, use_global_device_ids=true, to_apply=%region_1.0 | all-reduce | flops 12288 | bytes 49152 | tf_op jit(solution)/shard_map/psum | solution.py:110
  77.7 3.3 %all-to-all-start = ((bf16[1,64,4,2,128]{4,3,1,0,2:T(2,128)(2,1)}), bf16[1,64,4,2,128]{4,3,1,0,2:T(2,128)(2,1)S(1)}, u32[]{:S(2)}, u32[]{:S(2)}) async-start(bf16[1,64,4,2,128]{4,3,1,0,2:T(2,128)(2,1)} %copy.50), calls=%async_computation | async-start | bytes 262144 | tf_op jit(solution)/shard_map/all_to_all | solution.py:122
  81.1 0.2 reduce-scatter.2.cloned.1.call-start
  81.3 0.1 reshape.204
  81.5 0.2 fusion.14
  81.7 0.2 fusion.16
  81.9 0.2 subtract_convert_fusion
  82.1 0.1 maximum_convert_fusion
  82.2 4.7 %all-to-all-done = bf16[1,64,4,2,128]{4,3,1,0,2:T(2,128)(2,1)S(1)} async-done(((bf16[1,64,4,2,128]{4,3,1,0,2:T(2,128)(2,1)}), bf16[1,64,4,2,128]{4,3,1,0,2:T(2,128)(2,1)S(1)}, u32[]{:S(2)}, u32[]{:S(2)}) %all-to-all-start) | async-done | bytes 131104 | tf_op jit(solution)/shard_map/all_to_all | solution.py:122
  86.9 0.2 copy.51
  87.1 0.1 squeeze_reshape.9
  87.2 0.2 convolution_multiply_fusion.2
  87.4 8.8 %fusion.11 = f32[8,8,8,128]{3,1,2,0:T(8,128)S(1)} fusion(f32[64,1024]{1,0:T(8,128)S(1)} %convolution_multiply_fusion.2, bf16[64,8192]{1,0:T(8,128)(2,1)S(1)} %fusion.10, bf16[8192,1024]{1,0:T(8,128)(2,1)} %param.15), kind=kOutput, calls=%fused_computation.19 | convolution fusion | flops 1073807360 | bytes 18350080 | tf_op jit(solution)/shard_map/dot_general | solution.py:32
  96.2 0.2 multiply_subtract_fusion
  96.4 0.1 pad_maximum_fusion
  96.6 0.4 fusion.18
  97.0 0.1 copy.54
  97.1 8.5 %select_reduce_fusion = (f32[64,2,4]{2,1,0:T(2,128)S(1)}, f32[64,2,4,128]{3,2,1,0:T(4,128)S(1)}) fusion(pred[64,128]{1,0:T(8,128)(4,1)S(1)} %iota_compare_fusion, f32[64,2,4,128]{3,2,1,0:T(4,128)S(1)} %bitcast.58, bf16[64,2,128,128]{3,2,1,0:T(8,128)(2,1)} %param.23), kind=kOutput, calls=%fused_computation.34 | convolution fusion | flops 100859392 | bytes 4728832 | tf_op jit(solution)/shard_map/bkgd,bkld->bkgl/dot_general | solution.py:41
  105.6 0.1 copy.55
  105.7 0.1 copy.56
  105.8 0.4 fusion.19
  106.2 0.1 copy.57
  106.4 0.1 copy.58
  106.5 0.1 copy.59
  106.6 3.5 %fusion.12 = bf16[64,2,4,128]{3,2,1,0:T(4,128)(2,1)S(1)} fusion(bf16[64,2,128,128]{3,2,1,0:T(8,128)(2,1)} %param.24, f32[64,2,4,128]{3,2,1,0:T(4,128)S(1)} %get-tuple-element.16, f32[64,2,128]{2,1,0:T(2,128)S(1)} %reshape.192, f32[64,2,4]{2,1,0:T(2,128)S(1)} %copy.59, f32[64,2,4]{2,1,0:T(2,128)S(1)} %copy.58, f32[64,2,4]{2,1,0:T(2,128)S(1)} %copy.56, ...), kind=kOutput, calls=%fused_computation.20 | convolution fusion | flops 17235968 | bytes 4667392 | tf_op jit(solution)/shard_map/bkgl,bkld->bkgd/dot_general | solution.py:57
  110.1 0.1 reshape.189
  110.2 0.0 copy-start.1
  110.2 9.8 %convolution_convert_fusion = bf16[64,8192]{1,0:T(8,128)(2,1)} fusion(bf16[64,1024]{1,0:T(8,128)(2,1)S(1)} %reshape.189, bf16[1024,8192]{1,0:T(8,128)(2,1)} %param.17), kind=kOutput, calls=%fused_computation | convolution fusion | flops 1074266112 | bytes 17956864 | tf_op jit(solution)/shard_map/dot_general | solution.py:162
  120.0 0.0 reduce-scatter.2.cloned.1.call-update
  120.0 8.2 %all-gather.1 = bf16[64,1024]{1,0:T(8,128)(2,1)S(1)} all-gather(bf16[64,128]{1,0:T(8,128)(2,1)S(1)} %bitcast.66), channel_id=3, replica_groups=mesh['rep'=8,'tp'=4] {'rep'}, dimensions={1}, use_global_device_ids=true | all-gather | bytes 147456 | tf_op jit(solution)/shard_map/all_gather | solution.py:117
  128.2 0.1 reshape.190
  128.2 0.7 copy.61
  129.0 3.3 %all-to-all-start.2 = ((bf16[1,64,4,2,128]{4,3,1,0,2:T(2,128)(2,1)}), bf16[1,64,4,2,128]{4,3,1,0,2:T(2,128)(2,1)S(1)}, u32[]{:S(2)}, u32[]{:S(2)}) async-start(bf16[1,64,4,2,128]{4,3,1,0,2:T(2,128)(2,1)} %copy.61), calls=%async_computation.3 | async-start | bytes 262144 | tf_op jit(solution)/shard_map/all_to_all | solution.py:128
  132.3 9.8 %all-gather.2 = bf16[64,2048]{1,0:T(8,128)(2,1)S(1)} all-gather(bf16[64,256]{1,0:T(8,128)(2,1)S(1)} %copy-done.1), channel_id=4, replica_groups=mesh['rep'=8,'tp'=4] {'rep'}, dimensions={1}, use_global_device_ids=true | all-gather | bytes 294912 | tf_op jit(solution)/shard_map/all_gather | solution.py:118
  142.1 0.2 reshape.191
  142.2 0.9 copy.63
  143.1 5.0 %all-to-all-start.3 = ((bf16[1,64,4,2,256]{4,3,1,0,2:T(2,128)(2,1)}), bf16[1,64,4,2,256]{4,3,1,0,2:T(2,128)(2,1)S(1)}, u32[]{:S(2)}, u32[]{:S(2)}) async-start(bf16[1,64,4,2,256]{4,3,1,0,2:T(2,128)(2,1)} %copy.63), calls=%async_computation.4 | async-start | bytes 524288 | tf_op jit(solution)/shard_map/all_to_all | solution.py:131
  148.2 0.2 copy.62
  148.3 0.1 squeeze_reshape.10
  148.4 0.2 fusion.29
  148.6 19.5 %psum.15 = bf16[64,64]{1,0:T(8,128)(2,1)S(1)} all-reduce(f32[64,64]{1,0:T(8,128)S(1)} %fusion.29), channel_id=1, replica_groups=mesh['rep'=8,'tp'=4] {'tp'}, use_global_device_ids=true, to_apply=%region_6.7 | all-reduce | flops 4096 | bytes 24576 | tf_op jit(solution)/shard_map/psum | solution.py:161
  168.1 0.3 copy.64
  168.5 0.2 squeeze_reshape.11
  168.7 0.0 reduce-scatter.2.cloned.1.call-done
  168.7 1.9 %fusion.7 = bf16[64,2048]{1,0:T(8,128)(2,1)} fusion(bf16[64,2048]{1,0:T(8,128)(2,1)S(1)} %squeeze_reshape.11, bf16[64,2048]{1,0:T(8,128)(2,1)} %reduce-scatter.2.cloned.1.call-done, bf16[64,64]{1,0:T(8,128)(2,1)S(1)} %psum.15), kind=kOutput, calls=%fused_computation.11 | convolution fusion | flops 17301504 | bytes 794624 | tf_op jit(solution)/shard_map/dot_general | solution.py:166
  (24 shorter events, 0.2 us)
Async XLA Ops:
  18.2 59.5 %all-to-all-start.1 = ((bf16[4,2,4096]{2,1,0:T(2,128)(2,1)}), bf16[4,2,4096]{2,1,0:T(2,128)(2,1)S(1)}, u32[]{:S(2)}, u32[]{:S(2)}) async-start(bf16[4,2,4096]{2,1,0:T(2,128)(2,1)} %reshape.203), calls=%async_computation.1 | async-start | bytes 131072 | tf_op jit(solution)/shard_map/all_to_all | solution.py:125
  30.7 4.7 %copy-start = (bf16[3,256,64]{1,2,0:T(8,128)(2,1)S(1)}, bf16[3,256,64]{1,2,0:T(8,128)(2,1)}, u32[]{:S(2)}) copy-start(bf16[3,256,64]{1,2,0:T(8,128)(2,1)} %param.18) | copy-start | bytes 294916
  30.7 17.3 %copy-start.4 = (s32[64]{0:T(128)S(1)}, s32[64]{0:T(128)}, u32[]{:S(2)}) copy-start(s32[64]{0:T(128)} %param.25) | copy-start | bytes 772
  30.7 18.0 %copy-start.2 = (bf16[64,128]{1,0:T(8,128)(2,1)S(1)}, bf16[64,128]{1,0:T(8,128)(2,1)}, u32[]{:S(2)}) copy-start(bf16[64,128]{1,0:T(8,128)(2,1)} %param.19) | copy-start | bytes 49156
  77.7 9.2 %all-to-all-start = ((bf16[1,64,4,2,128]{4,3,1,0,2:T(2,128)(2,1)}), bf16[1,64,4,2,128]{4,3,1,0,2:T(2,128)(2,1)S(1)}, u32[]{:S(2)}, u32[]{:S(2)}) async-start(bf16[1,64,4,2,128]{4,3,1,0,2:T(2,128)(2,1)} %copy.50), calls=%async_computation | async-start | bytes 262144 | tf_op jit(solution)/shard_map/all_to_all | solution.py:122
  81.1 87.6 %reduce-scatter.2.cloned.1.call-start = ((), (), s32[]{:S(2)}) async-start(), calls=%async_computation.5 | async-start | bytes 1310720 | tf_op jit(solution)/shard_map/reduce_scatter | solution.py:163
  110.2 9.8 %copy-start.3 = (bf16[128,64]{0,1:T(8,128)(2,1)S(1)}, bf16[128,64]{0,1:T(8,128)(2,1)}, u32[]{:S(2)}) copy-start(bf16[128,64]{0,1:T(8,128)(2,1)} %param.21) | copy-start | bytes 49156
  110.2 22.1 %copy-start.1 = (bf16[64,256]{1,0:T(8,128)(2,1)S(1)}, bf16[64,256]{1,0:T(8,128)(2,1)}, u32[]{:S(2)}) copy-start(bf16[64,256]{1,0:T(8,128)(2,1)} %param.22) | copy-start | bytes 98308
  129.0 14.2 %all-to-all-start.2 = ((bf16[1,64,4,2,128]{4,3,1,0,2:T(2,128)(2,1)}), bf16[1,64,4,2,128]{4,3,1,0,2:T(2,128)(2,1)S(1)}, u32[]{:S(2)}, u32[]{:S(2)}) async-start(bf16[1,64,4,2,128]{4,3,1,0,2:T(2,128)(2,1)} %copy.61), calls=%async_computation.3 | async-start | bytes 262144 | tf_op jit(solution)/shard_map/all_to_all | solution.py:128
  143.1 25.0 %all-to-all-start.3 = ((bf16[1,64,4,2,256]{4,3,1,0,2:T(2,128)(2,1)}), bf16[1,64,4,2,256]{4,3,1,0,2:T(2,128)(2,1)S(1)}, u32[]{:S(2)}, u32[]{:S(2)}) async-start(bf16[1,64,4,2,256]{4,3,1,0,2:T(2,128)(2,1)} %copy.63), calls=%async_computation.4 | async-start | bytes 524288 | tf_op jit(solution)/shard_map/all_to_all | solution.py:131
Sparse Core Ops, SparseCore 0:
  120.1 27.4 reduce-scatter.1
where the time goes:
time: 178 us; the launch traced here: 177 us
  blocking collectives  89 us (50%)
  matrix products  39.5 us (22%)
  starting transfers between devices  16.8 us (9%)
  between operations  13.8 us (8%)
  local copies, waits for them, and re-layouts  7.97 us (4%)
  other arithmetic  5.58 us (3%)
  waiting for transfers between devices  4.78 us (3%)
    psum x1, blocking collectives, local(): inner = lax.psum(partial_inner.astype(jnp.bfloat16), 'tp')  19.8 us
    psum x1, blocking collectives, local(): middle = lax.psum(partial_middle, 'tp').astype(jnp.bfloat16)  19.5 us
    dot_general x3, matrix products, adapted(): jnp.dot(normed, frozen_matrix, preferred_element_type=jnp.float32)  14.8 us
    all_gather x1, blocking collectives, local(): lax.all_gather(input_down_factors, 'rep', axis=1, tiled=True)  12.6 us
    all_gather x1, blocking collectives, local(): lax.all_gather(key_value_up_factors, 'rep', axis=2, tiled=True)  10.9 us
    dot_general x1, matrix products, local(): jnp.dot(context, output_weight_matrix, preferred_element_type=jnp.float32)  9.79 us
    all_gather x1, blocking collectives, local(): lax.all_gather(out_up_rows, 'rep', axis=2, tiled=True)  9.75 us
    dot_general x1, matrix products, attend(): jnp.einsum('bkgd,bkld->bkgl', query, keys.astype(jnp.float32), precision=...  8.5 us
  transfers between devices with their start and end apart: 5, of which 1 were waited for; matrix products, arithmetic and copies ran while one was open for 10% of the time, Pallas kernels for 0%

commit v1 on v0

v1 whole, which is shorter than its diff:
```python
import functools
import math

import jax
import jax.numpy as jnp
from jax import lax
from jax.experimental import pallas as pl
from jax.experimental.pallas import tpu as pltpu
from jax.sharding import PartitionSpec as P

epsilon = 1e-06
rope_base = 1000000.0
adapter_scale = 0.5

f32 = jnp.float32
bf16 = jnp.bfloat16
LANES = 128
MESH_ID = pl.DeviceIdType.MESH


def nt_dot(left, right):
    return lax.dot_general(
        left, right, (((1,), (1,)), ((), ())), preferred_element_type=f32
    )


def nn_dot(left, right):
    return jnp.dot(left, right, preferred_element_type=f32)


def channels_of(n):
    return ((1, 0, n // 2), (-1, 1, n // 2), (1, 1, n // 2 - 1), (-1, 0, n // 2 - 1))


def kernel(
    dims,
    hidden,
    gain,
    wq,
    wkv,
    wo,
    dn_own,
    v_own,
    cache_k,
    cache_v,
    lengths,
    cos,
    sin,
    out,
    hid_b,
    norm_b,
    wq_b,
    wkv_b,
    wo_b,
    k_b,
    v_b,
    dn_b,
    vo_b,
    vf_b,
    q_acc,
    kv_acc,
    inner_s,
    inner_r,
    q3,
    nk3,
    nv3,
    c3,
    ctx,
    mid_s,
    mid_r,
    rs_s,
    rs_r,
    hid_sem,
    w_sem,
    kv_sem,
    wo_sem,
    k_sem,
    v_sem,
    own_sem,
    dn_ssem,
    dn_rsem,
    dn_fsem,
    vf_ssem,
    vf_rsem,
    vf_fsem,
    in_ssem,
    in_rsem,
    mid_ssem,
    mid_rsem,
    rs_ssem,
    rs_rsem,
):
    n, reps = dims["tp"], dims["rep"]
    seqs, depth = hidden.shape
    head_dim = cache_k.shape[3]
    kv_local = cache_k.shape[1]
    heads = wq.shape[1] // head_dim
    group = heads // kv_local
    pad_heads = q3.shape[0] // seqs
    rank = dims["rank"]
    block, win = dims["block"], dims["win"]
    q_rows, up_rows, kv_rows = dims["q_rows"], dims["up_rows"], dims["kv_rows"]
    half_reps = reps // 2
    r = lax.axis_index("rep")
    t = lax.axis_index("tp")
    core = lax.rem(r, 2)
    partner = r + 1 - 2 * core

    own_dn = pltpu.make_async_copy(dn_own, dn_b.at[r], own_sem.at[0])
    own_v = pltpu.make_async_copy(v_own, vo_b, own_sem.at[1])
    own_dn.start()
    own_v.start()
    hid = pltpu.make_async_copy(hidden, hid_b, hid_sem)
    hid.start()
    steps = w_sem.shape[0]
    kc = depth // steps

    def w_copies(i):
        rows = pl.ds(pl.multiple_of(i * kc, kc), kc)
        return (
            pltpu.make_async_copy(wq.at[rows, :], wq_b.at[rows, :], w_sem.at[i]),
            pltpu.make_async_copy(wkv.at[:, rows, :], wkv_b.at[:, rows, :], kv_sem.at[i]),
        )

    @pl.loop(0, steps)
    def _(i):
        for c in w_copies(i):
            c.start()

    parts = k_sem.shape[0]
    ps = seqs // parts

    def cache_copies(i):
        rows = pl.ds(i * ps, ps)
        return (
            pltpu.make_async_copy(cache_k.at[rows], k_b.at[rows], k_sem.at[i]),
            pltpu.make_async_copy(cache_v.at[rows], v_b.at[rows], v_sem.at[i]),
        )

    @pl.loop(0, parts)
    def _(i):
        for c in cache_copies(i):
            c.start()

    wide = wo.shape[1] // n
    half_w = wide // 2

    def out_cols(k, half):
        d = lax.rem(t + k + n, n)
        return pl.ds(pl.multiple_of(d * wide + half * half_w, LANES), half_w)

    def wo_copy(k, half):
        cols = out_cols(k, half)
        idx = (k % n) * 2 + half
        return pltpu.make_async_copy(wo.at[:, cols], wo_b.at[idx], wo_sem.at[idx])

    sends = []
    for k in range(n // 2, 0, -1):
        for fresh in (True, False):
            for ci, (way, half, hops) in enumerate(channels_of(n)):
                if k <= hops and (k == hops) == fresh:
                    sends.append((ci, way, half, hops, k))
    for _ci, way, half, _hops, k in sends:
        wo_copy(way * k, half).start()
    wo_copy(0, 0).start()
    wo_copy(0, 1).start()

    flat = r * n + t
    plane = flat // reps
    slot = lax.rem(flat, reps)
    barrier = pltpu.get_barrier_semaphore()

    def greet(rr, tt):
        pl.semaphore_signal(barrier, inc=1, device_id=(rr, tt), device_id_type=MESH_ID)

    count = 0
    greet(partner, t)
    count += 1
    for j in range(1, n):
        greet(r, lax.rem(t + j, n))
        count += 1
    for j in range(1, half_reps):
        greet(lax.rem(r + 2 * j, reps), t)
        count += 1
        greet(lax.rem(r + 2 * j, reps), plane)
        count += 1

    greet(jnp.where(plane == t, partner, r), plane)
    count += 1
    groups = reps // n // 2

    def source_of(i, z):
        s = n * (2 * i + core) + z
        return s, (reps * t + s) // n

    for i in range(groups):
        for z in range(n):
            _s, sr = source_of(i, z)
            same = jnp.logical_and(sr == r, t == z)
            greet(jnp.where(same, partner, sr), z)
            count += 1
    pl.semaphore_wait(barrier, count)

    def remote(src, dst, ssem, rsem, rr, tt):
        return pltpu.make_async_remote_copy(
            src_ref=src,
            dst_ref=dst,
            send_sem=ssem,
            recv_sem=rsem,
            device_id=(rr, tt),
            device_id_type=MESH_ID,
        )

    own_dn.wait()
    dn_sends = []
    for j in range(1, half_reps):
        dn_sends.append(
            remote(
                dn_b.at[r], dn_b.at[r], dn_ssem.at[j], dn_rsem.at[r],
                lax.rem(r + 2 * j, reps), t,
            )
        )
    dn_sends.append(
        remote(dn_b.at[r], dn_b.at[r], dn_fsem.at[0], dn_rsem.at[r], partner, t)
    )
    for c in dn_sends:
        c.start()
    own_v.wait()
    v_sends = [
        remote(
            vo_b, vf_b.at[slot], vf_ssem.at[j], vf_rsem.at[slot],
            lax.rem(r + 2 * j, reps), plane,
        )
        for j in range(half_reps)
    ]
    v_home = pltpu.make_async_copy(vo_b, vf_b.at[slot], vf_rsem.at[slot])
    for j in range(1, half_reps):
        v_sends[j].start()

    @pl.when(plane != t)
    def _():
        v_sends[0].start()

    @pl.when(plane == t)
    def _():
        v_home.start()

    hid.wait()

    @pl.loop(0, seqs // 16)
    def _(i):
        rows = pl.ds(pl.multiple_of(i * 16, 16), 16)
        x = hid_b[rows, :].astype(f32)
        square = jnp.mean(x * x, axis=-1, keepdims=True)
        norm_b[rows, :] = (
            x * lax.rsqrt(square + epsilon) * gain[...].astype(f32)
        ).astype(bf16)

    q_acc[...] = jnp.zeros_like(q_acc)
    kv_acc[...] = jnp.zeros_like(kv_acc)

    def project(lo, hi):
        @pl.loop(lo, hi)
        def _(i):
            for c in w_copies(i):
                c.wait()
            rows = pl.ds(pl.multiple_of(i * kc, kc), kc)
            x = norm_b[:, rows]
            q_acc[...] += nn_dot(x, wq_b[rows, :])
            for j in range(2):
                kv_acc[j] += nn_dot(x, wkv_b[j, rows, :])

    project(0, steps // 2)

    dn_fwd = []
    for j in range(half_reps - 1, 0, -1):
        src = lax.rem(r + 2 * j, reps)
        remote(dn_b.at[src], dn_b.at[src], dn_fsem.at[j], dn_rsem.at[src], partner, t).wait_recv()
        c = remote(dn_b.at[src], dn_b.at[src], dn_fsem.at[j], dn_rsem.at[src], partner, t)
        c.start()
        dn_fwd.append(c)
    for j in range(half_reps):
        src = lax.rem(partner + 2 * j, reps)
        remote(dn_b.at[src], dn_b.at[src], dn_fsem.at[j], dn_rsem.at[src], partner, t).wait_recv()

    part = jnp.zeros((seqs, 3 * rank), f32)
    for j in range(reps):
        start = (j * n + t) * block
        cols = pl.ds(pl.multiple_of(start // win * win, LANES), win)
        part = part + nt_dot(norm_b[:, cols], dn_b[j])
    inner_s[...] = part
    in_sends = []
    for j in range(1, n):
        c = remote(
            inner_s, inner_r.at[j], in_ssem.at[j], in_rsem.at[j], r, lax.rem(t + j, n)
        )
        c.start()
        in_sends.append(c)

    project(steps // 2, steps)

    v_fwd = []
    for i in range(groups):
        for z in range(n):
            s, _sr = source_of(i, z)
            pltpu.make_async_copy(vo_b, vf_b.at[s], vf_rsem.at[s]).wait()
            c = remote(
                vf_b.at[s], vf_b.at[s], vf_fsem.at[i * n + z], vf_rsem.at[s], partner, t
            )
            c.start()
            v_fwd.append(c)
    for i in range(groups):
        for z in range(n):
            s = n * (2 * i + 1 - core) + z
            pltpu.make_async_copy(vo_b, vf_b.at[s], vf_rsem.at[s]).wait()

    total = inner_s[...]
    for c in in_sends:
        c.wait_recv()
    for j in range(1, n):
        total = total + inner_r[j]
    inner = total.astype(bf16).astype(f32)
    lane = lax.broadcasted_iota(jnp.int32, (seqs, 2 * rank), 1)
    first = inner[:, : 2 * rank]
    inner_q = jnp.where(lane < rank, first, 0.0).astype(bf16)
    inner_k = jnp.where(lane < rank, 0.0, first).astype(bf16)
    inner_v = inner[:, 2 * rank :].astype(bf16)

    q_od = vf_b[:, :q_rows, :].reshape(reps * q_rows, 2 * rank)
    kv_up = (
        vf_b[:, q_rows + up_rows :, :]
        .astype(f32)
        .reshape(reps * kv_rows, 2 * rank)
        .astype(bf16)
    )
    q = q_acc[...] + adapter_scale * nt_dot(inner_q, q_od)
    nk = kv_acc[0] + adapter_scale * nt_dot(inner_k, kv_up)
    nv = kv_acc[1] + adapter_scale * nt_dot(inner_v, kv_up[:, :rank])

    cosv, sinv = cos[...], sin[...]

    def turn(x):
        return x * cosv + pltpu.roll(x, head_dim // 2, 1) * sinv

    for h in range(pad_heads):
        rows = pl.ds(h, seqs, stride=pad_heads)
        if h < heads:
            q3[rows, :] = turn(q[:, h * head_dim : (h + 1) * head_dim])
        else:
            q3[rows, :] = jnp.zeros((seqs, head_dim), f32)
    for j in range(kv_local):
        key = turn(nk[:, j * head_dim : (j + 1) * head_dim]).astype(bf16).astype(f32)
        val = nv[:, j * head_dim : (j + 1) * head_dim].astype(bf16).astype(f32)
        for g in range(pad_heads):
            if min(g // group, kv_local - 1) == j:
                rows = pl.ds(g, seqs, stride=pad_heads)
                nk3[rows, :] = key
                nv3[rows, :] = val

    cache = cache_k.shape[2]
    span = kv_local * cache
    score_scale = 1.0 / math.sqrt(head_dim)
    bs = 8
    per = ps // bs

    @pl.loop(0, seqs // bs)
    def _(i):
        @pl.when(lax.rem(i, per) == 0)
        def _():
            for c in cache_copies(i // per):
                c.wait()

        base = pl.multiple_of(i * (bs * pad_heads), bs * pad_heads)
        rows = pl.ds(base, bs * pad_heads)
        qq = q3[rows, :]
        hi = qq.astype(bf16).astype(f32)
        rest = qq - hi
        mid = rest.astype(bf16).astype(f32)
        low = rest - mid
        own = jnp.sum(qq * nk3[rows, :], axis=-1, keepdims=True) * score_scale
        row_id = lax.broadcasted_iota(jnp.int32, (pad_heads, span), 0)
        col_id = lax.broadcasted_iota(jnp.int32, (pad_heads, span), 1)
        mine = jnp.minimum(row_id // group, kv_local - 1) == col_id // cache
        pos = lax.rem(col_id, cache)
        for b in range(bs):
            sl = slice(b * pad_heads, (b + 1) * pad_heads)
            stack = jnp.concatenate([hi[sl], mid[sl], low[sl]], axis=0).astype(bf16)
            keys = k_b[i * bs + b].reshape(span, head_dim)
            dots = nt_dot(stack, keys)
            sc = (
                dots[:pad_heads]
                + dots[pad_heads : 2 * pad_heads]
                + dots[2 * pad_heads :]
            ) * score_scale
            live = jnp.logical_and(mine, pos < lengths[i * bs + b])
            top = jnp.maximum(
                jnp.max(jnp.where(live, sc, -1e30), axis=-1, keepdims=True), own[sl]
            )
            w = jnp.where(live, jnp.exp(sc - top), 0.0)
            ow = jnp.exp(own[sl] - top)
            denom = jnp.sum(w, axis=-1, keepdims=True) + ow
            probs = (w / denom).astype(bf16)
            own_p = (ow / denom).astype(bf16).astype(f32)
            vals = v_b[i * bs + b].reshape(span, head_dim)
            here = pl.ds(base + b * pad_heads, pad_heads)
            c3[here, :] = nn_dot(probs, vals) + own_p * nv3[here, :]

    for h in range(heads):
        ctx[:, h * head_dim : (h + 1) * head_dim] = c3[
            pl.ds(h, seqs, stride=pad_heads), :
        ].astype(bf16)

    mid_s[...] = nn_dot(ctx[...], q_od)
    mid_sends = []
    for j in range(1, n):
        c = remote(mid_s, mid_r.at[j], mid_ssem.at[j], mid_rsem.at[j], r, lax.rem(t + j, n))
        c.start()
        mid_sends.append(c)

    tile = min(512, half_w)
    offsets = []
    at = 0
    for _way, _half, hops in channels_of(n):
        offsets.append(at)
        at += hops
    rs_sends = []
    for ci, way, half, hops, k in sends:
        idx = ((way * k) % n) * 2 + half
        wo_copy(way * k, half).wait()
        place = offsets[ci] + k - 1
        if k < hops:
            remote(
                rs_s.at[place + 1], rs_r.at[place + 1], rs_ssem.at[place + 1],
                rs_rsem.at[place + 1], r, lax.rem(t + way + n, n),
            ).wait_recv()

        @pl.loop(0, half_w // tile)
        def _(i):
            cols = pl.ds(pl.multiple_of(i * tile, tile), tile)
            value = nn_dot(ctx[...], wo_b[idx, :, cols])
            if k < hops:
                value = value + rs_r[place + 1, :, cols].astype(f32)
            rs_s[place, :, cols] = value.astype(bf16)

        c = remote(
            rs_s.at[place], rs_r.at[place], rs_ssem.at[place], rs_rsem.at[place],
            r, lax.rem(t + way + n, n),
        )
        c.start()
        rs_sends.append((c, k))

    total_mid = mid_s[:, rank:]
    for c in mid_sends:
        c.wait_recv()
    for j in range(1, n):
        total_mid = total_mid + mid_r[j][:, rank:]
    middle = total_mid.astype(bf16)
    ups = vf_b[:, q_rows : q_rows + up_rows, :].astype(f32)
    up_full = (
        jnp.concatenate([ups[:, :, :rank], ups[:, :, rank:]], axis=1)
        .reshape(reps * 2 * up_rows, rank)
        .astype(bf16)
    )
    final = []
    for half in range(2):
        wo_copy(0, half).wait()
        final.append(
            nn_dot(ctx[...], wo_b[half])
            + adapter_scale * nt_dot(middle, up_full[half * half_w : (half + 1) * half_w])
        )
    for c, k in rs_sends:
        if k == 1:
            c.wait_recv()
    for half in range(2):
        value = final[half]
        for ci, (_way, h2, hops) in enumerate(channels_of(n)):
            if h2 == half and hops > 0:
                value = value + rs_r[offsets[ci]].astype(f32)
        out[:, half * half_w : (half + 1) * half_w] = value.astype(bf16)

    for c in dn_sends + dn_fwd + v_fwd + in_sends + mid_sends:
        c.wait_send()
    for j in range(1, half_reps):
        v_sends[j].wait_send()

    @pl.when(plane != t)
    def _():
        v_sends[0].wait_send()

    for c, _k in rs_sends:
        c.wait_send()


def local(
    hidden,
    norm_gain,
    query_weight_matrix,
    key_value_weight,
    output_weight_matrix,
    input_down_factors,
    query_up_factor,
    key_value_up_factors,
    output_down_factor,
    output_up_factor,
    cache_keys,
    cache_values,
    lengths,
):
    reps, n = lax.axis_size("rep"), lax.axis_size("tp")
    r, t = lax.axis_index("rep"), lax.axis_index("tp")
    seqs, depth = hidden.shape
    _, kv_local, cache, head_dim = cache_keys.shape
    width = query_weight_matrix.shape[1]
    heads = width // head_dim
    rank = input_down_factors.shape[2]
    block = input_down_factors.shape[1]
    win = max(block, LANES)

    down = jnp.swapaxes(input_down_factors, 1, 2).reshape(3 * rank, block)
    if win != block:
        spot = lax.rem((r * n + t) * block, win)
        down = lax.dynamic_update_slice(
            jnp.zeros((3 * rank, win), down.dtype), down, (0, spot)
        )
    q_rows = query_up_factor.shape[1]
    kv_rows = key_value_up_factors.shape[2]
    up = output_up_factor.T
    up_rows = up.shape[0] // 2
    packed = jnp.concatenate(
        [
            jnp.concatenate([query_up_factor.T, output_down_factor], axis=1),
            jnp.concatenate([up[:up_rows], up[up_rows:]], axis=1),
            jnp.concatenate([key_value_up_factors[1].T, key_value_up_factors[0].T], axis=1),
        ],
        axis=0,
    )
    half_dim = head_dim // 2
    frequency = rope_base ** (-(jnp.arange(half_dim, dtype=f32) * 2.0) / head_dim)
    angles = lengths.astype(f32)[:, None] * frequency[None, :]
    cosine, sine = jnp.cos(angles), jnp.sin(angles)
    cos2 = jnp.concatenate([cosine, cosine], axis=1)
    sin2 = jnp.concatenate([-sine, sine], axis=1)

    dims = dict(
        tp=n, rep=reps, rank=rank, block=block, win=win,
        q_rows=q_rows, up_rows=up_rows, kv_rows=kv_rows,
    )
    pad_heads = -(-heads // 8) * 8
    wide = depth // n
    half_w = wide // 2
    rows = seqs * pad_heads
    slots = sum(hops for _, _, hops in channels_of(n))
    steps, parts = 16, 4
    dma = pltpu.SemaphoreType.DMA
    hbm = pl.BlockSpec(memory_space=pl.ANY)
    vmem = pl.BlockSpec(memory_space=pltpu.VMEM)
    smem = pl.BlockSpec(memory_space=pltpu.SMEM)
    vec = pltpu.VMEM
    return pl.pallas_call(
        functools.partial(kernel, dims),
        name="decode_block",
        out_shape=jax.ShapeDtypeStruct((seqs, wide), bf16),
        in_specs=[hbm, vmem, hbm, hbm, hbm, hbm, hbm, hbm, hbm, smem, vmem, vmem],
        out_specs=vmem,
        scratch_shapes=[
            vec((seqs, depth), bf16),
            vec((seqs, depth), bf16),
            vec((depth, width), bf16),
            vec((2, depth, kv_local * head_dim), bf16),
            vec((2 * n, width, half_w), bf16),
            vec((seqs, kv_local, cache, head_dim), bf16),
            vec((seqs, kv_local, cache, head_dim), bf16),
            vec((reps, 3 * rank, win), bf16),
            vec(packed.shape, bf16),
            vec((reps,) + packed.shape, bf16),
            vec((seqs, width), f32),
            vec((2, seqs, kv_local * head_dim), f32),
            vec((seqs, 3 * rank), f32),
            vec((n, seqs, 3 * rank), f32),
            vec((rows, head_dim), f32),
            vec((rows, head_dim), f32),
            vec((rows, head_dim), f32),
            vec((rows, head_dim), f32),
            vec((seqs, width), bf16),
            vec((seqs, 2 * rank), f32),
            vec((n, seqs, 2 * rank), f32),
            vec((slots, seqs, half_w), bf16),
            vec((slots, seqs, half_w), bf16),
            dma,
            dma((steps,)),
            dma((steps,)),
            dma((2 * n,)),
            dma((parts,)),
            dma((parts,)),
            dma((2,)),
            dma((reps // 2,)),
            dma((reps,)),
            dma((reps // 2,)),
            dma((reps // 2,)),
            dma((reps,)),
            dma((reps // 2,)),
            dma((n,)),
            dma((n,)),
            dma((n,)),
            dma((n,)),
            dma((slots,)),
            dma((slots,)),
        ],
        compiler_params=pltpu.CompilerParams(
            collective_id=0, has_side_effects=True, vmem_limit_bytes=66000000
        ),
    )(
        hidden,
        norm_gain.reshape(1, -1),
        query_weight_matrix,
        key_value_weight,
        output_weight_matrix,
        down,
        packed,
        cache_keys,
        cache_values,
        lengths,
        cos2,
        sin2,
    )


def solution(mesh):
    return jax.shard_map(
        local,
        mesh=mesh,
        in_specs=(
            P("rep", None),
            P(),
            P(None, "tp"),
            P(None, None, "tp"),
            P("tp", None),
            P(None, ("rep", "tp"), None),
            P(None, ("rep", "tp")),
            P(None, None, ("rep", "tp")),
            P(("rep", "tp"), None),
            P(None, ("rep", "tp")),
            P("rep", "tp", None, None),
            P("rep", "tp", None, None),
            P("rep"),
        ),
        out_specs=P("rep", "tp"),
        check_vma=False,
    )
```

time: 178 us -> 84 us (0.47)
  blocking collectives: 89 us -> 0 us
  Pallas kernels: 0 us -> 74.9 us
  matrix products: 39.5 us -> 0 us
  starting transfers between devices: 16.8 us -> 0 us
  between operations: 13.8 us -> 0.03 us
  waiting for transfers between devices: 4.78 us -> 0 us
  other arithmetic: 5.58 us -> 2.3 us
    pallas_call x0 -> x1, Pallas kernels: none -> 74.9 us  [local(): pl.pallas_call(functools.partial(kernel, dims), name='decode_block', out_...]
    all_gather x5 -> x0, blocking collectives: 49.6 us -> none  [the longest x1 12.6 us: local(): lax.all_gather(input_down_factors, 'rep', axis=1, tiled=True)]
    dot_general x12 -> x0, matrix products: 39.5 us -> none  [the longest x3 14.8 us: adapted(): jnp.dot(normed, frozen_matrix, preferred_element_type=jnp.float32)]
    psum x2 -> x0, blocking collectives: 39.4 us -> none  [the longest x1 19.8 us: local(): inner = lax.psum(partial_inner.astype(jnp.bfloat16), 'tp')]
    all_to_all x4 -> x0, starting transfers between devices: 16.6 us -> none  [the longest x1 5.03 us: local(): lax.all_to_all(regroup(per_rep[3], tp_count, group), 'tp', split_axis=2,...]
    all_to_all x4 -> x0, waiting for transfers between devices: 4.74 us -> none  [the longest x1 4.73 us: local(): lax.all_to_all(regroup(per_rep[0], tp_count, group), 'tp', split_axis=2,...]
    unnamed x13 -> x4, local copies, waits for them, and re-layouts: 1.01 us -> 4.21 us
    reduce_sum x3 -> x0, other arithmetic: 2.39 us -> none  [the longest x1 1.53 us: local(): square = jnp.mean(states * states, axis=-1, keepdims=True)]
  transfers between devices with their start and end apart: 5 -> 0, of which waited for: 1 -> 0; matrix products, arithmetic and copies ran while one was open for 10% -> 0% of each run, Pallas kernels for 0% -> 0%
where the time goes in v1:
time: 84 us; the launch traced here: 83.5 us
  Pallas kernels  74.9 us (89%)
  local copies, waits for them, and re-layouts  6.28 us (7%)
  other arithmetic  2.3 us (3%)
    pallas_call x1, Pallas kernels, local(): pl.pallas_call(functools.partial(kernel, dims), name='decode_block', out_...  74.9 us
    unnamed x4, local copies, waits for them, and re-layouts  4.21 us

profile of v1, /device:TPU:0, one launch (start us, length us, event | category | flops | bytes accessed | tf_op | source)
XLA Modules:
  0.0 83.5 jit_solution(7287281738742040434)
XLA Ops:
  0.0 0.7 convert_element_type.3
  0.7 0.7 slice_bitcast_fusion.1
  1.4 1.3 %reshape.14.gain = bf16[1,8192]{1,0:T(2,128)(2,1)} reshape(bf16[8192]{0:T(1024)(128)(2,1)} %param.14) | data formatting | bytes 32768 | tf_op jit(solution)/shard_map/reshape | solution.py:614
  2.7 0.8 copy.14
  3.6 0.8 copy.15
  4.4 0.9 %copy.16 = bf16[64,256]{0,1:T(8,128)(2,1)S(1)} copy(bf16[64,256]{1,0:T(8,128)(2,1)} %param.22) | data formatting | bytes 65536 | tf_op args[9]
  5.3 0.7 maximum_maximum_fusion.v_own
  6.0 0.2 fusion
  6.2 0.7 pad_maximum_fusion
  6.9 74.9 %decode_block.1 = bf16[64,2048]{1,0:T(8,128)(2,1)} custom-call(bf16[64,8192]{1,0:T(8,128)(2,1)} %hidden.1, bf16[1,8192]{1,0:T(2,128)(2,1)} %reshape.14.gain, bf16[8192,1024]{1,0:T(8,128)(2,1)} %wq.1, bf16[2,8192,256]{2,1,0:T(8,128)(2,1)} %wkv.1, bf16[1024,8192]{1,0:T(8,128)(2,1)} %wo.1, bf16[192,256]{1,0:T(8,128)(2,1)} %bitcast.15, ...), custom_call_target="tpu_custom_call" | custom-call | tf_op jit(solution)/shard_map/decode_block/pallas_call | solution.py:559
  81.8 1.7 %copy.18 = bf16[64,2048]{1,0:T(8,128)(2,1)} copy(bf16[64,2048]{1,0:T(8,128)(2,1)} %decode_block.1) | data formatting | bytes 524288
  (2 shorter events, 0.0 us)

commit v2 on v1

--- a/solution.py
+++ b/solution.py
@@ -40,12 +40,13 @@
     wkv,
     wo,
     dn_own,
-    v_own,
+    f_q,
+    f_kv,
+    f_od,
+    f_ou,
     cache_k,
     cache_v,
     lengths,
-    cos,
-    sin,
     out,
     hid_b,
     norm_b,
@@ -55,8 +56,15 @@
     k_b,
     v_b,
     dn_b,
-    vo_b,
-    vf_b,
+    a_q,
+    a_kv,
+    a_od,
+    a_ou,
+    g_q,
+    g_kv,
+    g_od,
+    g_ou,
+    angle,
     q_acc,
     kv_acc,
     inner_s,
@@ -80,9 +88,11 @@
     dn_ssem,
     dn_rsem,
     dn_fsem,
-    vf_ssem,
-    vf_rsem,
-    vf_fsem,
+    a_ssem,
+    a_rsem,
+    g_ssem,
+    g_rsem,
+    g_fsem,
     in_ssem,
     in_rsem,
     mid_ssem,
@@ -99,7 +109,6 @@
     pad_heads = q3.shape[0] // seqs
     rank = dims["rank"]
     block, win = dims["block"], dims["win"]
-    q_rows, up_rows, kv_rows = dims["q_rows"], dims["up_rows"], dims["kv_rows"]
     half_reps = reps // 2
     r = lax.axis_index("rep")
     t = lax.axis_index("tp")
@@ -107,9 +116,16 @@
     partner = r + 1 - 2 * core
 
     own_dn = pltpu.make_async_copy(dn_own, dn_b.at[r], own_sem.at[0])
-    own_v = pltpu.make_async_copy(v_own, vo_b, own_sem.at[1])
+    mine_at = r // 2
+    spread = (a_q, a_kv, a_od, a_ou)
+    gathered = (g_q, g_kv, g_od, g_ou)
+    own_f = [
+        pltpu.make_async_copy(src, dst.at[mine_at], own_sem.at[1 + f])
+        for f, (src, dst) in enumerate(zip((f_q, f_kv, f_od, f_ou), spread))
+    ]
     own_dn.start()
-    own_v.start()
+    for c in own_f:
+        c.start()
     hid = pltpu.make_async_copy(hidden, hid_b, hid_sem)
     hid.start()
     steps = w_sem.shape[0]
@@ -165,9 +181,6 @@
     wo_copy(0, 0).start()
     wo_copy(0, 1).start()
 
-    flat = r * n + t
-    plane = flat // reps
-    slot = lax.rem(flat, reps)
     barrier = pltpu.get_barrier_semaphore()
 
     def greet(rr, tt):
@@ -182,23 +195,7 @@
     for j in range(1, half_reps):
         greet(lax.rem(r + 2 * j, reps), t)
         count += 1
-        greet(lax.rem(r + 2 * j, reps), plane)
-        count += 1
-
-    greet(jnp.where(plane == t, partner, r), plane)
-    count += 1
-    groups = reps // n // 2
-
-    def source_of(i, z):
-        s = n * (2 * i + core) + z
-        return s, (reps * t + s) // n
-
-    for i in range(groups):
-        for z in range(n):
-            _s, sr = source_of(i, z)
-            same = jnp.logical_and(sr == r, t == z)
-            greet(jnp.where(same, partner, sr), z)
-            count += 1
+
     pl.semaphore_wait(barrier, count)
 
     def remote(src, dst, ssem, rsem, rr, tt):
@@ -225,25 +222,70 @@
     )
     for c in dn_sends:
         c.start()
-    own_v.wait()
-    v_sends = [
-        remote(
-            vo_b, vf_b.at[slot], vf_ssem.at[j], vf_rsem.at[slot],
-            lax.rem(r + 2 * j, reps), plane,
-        )
-        for j in range(half_reps)
-    ]
-    v_home = pltpu.make_async_copy(vo_b, vf_b.at[slot], vf_rsem.at[slot])
-    for j in range(1, half_reps):
-        v_sends[j].start()
-
-    @pl.when(plane != t)
-    def _():
-        v_sends[0].start()
-
-    @pl.when(plane == t)
-    def _():
-        v_home.start()
+    a_sends = []
+    for f, buf in enumerate(spread):
+        own_f[f].wait()
+        for j in range(1, half_reps):
+            c = remote(
+                buf.at[mine_at], buf.at[mine_at], a_ssem.at[f, j], a_rsem.at[f, mine_at],
+                lax.rem(r + 2 * j, reps), t,
+            )
+            c.start()
+            a_sends.append(c)
+
+    per_plane = reps // n
+    groups = per_plane // 2
+    g_sends = []
+
+    def to_planes(f):
+        buf, full = spread[f], gathered[f]
+        for j in range(1, half_reps):
+            src = lax.rem(r + 2 * j, reps) // 2
+            remote(
+                buf.at[src], buf.at[src], a_ssem.at[f, j], a_rsem.at[f, src], r, t
+            ).wait_recv()
+        for i in range(groups):
+            s = n * (2 * i + core) + t
+            for j in range(1, n):
+                plane = lax.rem(t + j, n)
+                src = (plane * per_plane + 2 * i) // 2
+                c = remote(
+                    buf.at[src], full.at[s], g_ssem.at[f, i * n + j], g_rsem.at[f, s],
+                    r, plane,
+                )
+                c.start()
+                g_sends.append(c)
+            src = (t * per_plane + 2 * i) // 2
+            pltpu.make_async_copy(buf.at[src], full.at[s], g_rsem.at[f, s]).start()
+
+    def across(f):
+        full = gathered[f]
+        for i in range(groups):
+            for z in range(n):
+                s = n * (2 * i + core) + z
+                pltpu.make_async_copy(spread[f].at[0], full.at[s], g_rsem.at[f, s]).wait()
+                c = remote(
+                    full.at[s], full.at[s], g_fsem.at[f, i * n + z], g_rsem.at[f, s],
+                    partner, t,
+                )
+                c.start()
+                g_sends.append(c)
+
+    def settled(f):
+        full = gathered[f]
+        for i in range(groups):
+            for z in range(n):
+                s = n * (2 * i + 1 - core) + z
+                pltpu.make_async_copy(spread[f].at[0], full.at[s], g_rsem.at[f, s]).wait()
+
+    half_dim = head_dim // 2
+    step = lax.rem(lax.broadcasted_iota(jnp.int32, (1, head_dim), 1), half_dim)
+    frequency = jnp.exp(step.astype(f32) * (-2.0 * math.log(rope_base) / head_dim))
+
+    @pl.loop(0, seqs // 8)
+    def _(i):
+        for b in range(8):
+            angle[pl.ds(i * 8 + b, 1), :] = lengths[i * 8 + b].astype(f32) * frequency
 
     hid.wait()
 
@@ -270,7 +312,10 @@
             for j in range(2):
                 kv_acc[j] += nn_dot(x, wkv_b[j, rows, :])
 
-    project(0, steps // 2)
+    project(0, steps // 4)
+    to_planes(0)
+    to_planes(1)
+    project(steps // 4, steps // 2)
 
     dn_fwd = []
     for j in range(half_reps - 1, 0, -1):
@@ -297,22 +342,13 @@
         c.start()
         in_sends.append(c)
 
+    across(0)
+    across(1)
+    to_planes(2)
+    to_planes(3)
     project(steps // 2, steps)
-
-    v_fwd = []
-    for i in range(groups):
-        for z in range(n):
-            s, _sr = source_of(i, z)
-            pltpu.make_async_copy(vo_b, vf_b.at[s], vf_rsem.at[s]).wait()
-            c = remote(
-                vf_b.at[s], vf_b.at[s], vf_fsem.at[i * n + z], vf_rsem.at[s], partner, t
-            )
-            c.start()
-            v_fwd.append(c)
-    for i in range(groups):
-        for z in range(n):
-            s = n * (2 * i + 1 - core) + z
-            pltpu.make_async_copy(vo_b, vf_b.at[s], vf_rsem.at[s]).wait()
+    settled(0)
+    settled(1)
 
     total = inner_s[...]
     for c in in_sends:
@@ -320,24 +356,26 @@
     for j in range(1, n):
         total = total + inner_r[j]
     inner = total.astype(bf16).astype(f32)
-    lane = lax.broadcasted_iota(jnp.int32, (seqs, 2 * rank), 1)
-    first = inner[:, : 2 * rank]
-    inner_q = jnp.where(lane < rank, first, 0.0).astype(bf16)
-    inner_k = jnp.where(lane < rank, 0.0, first).astype(bf16)
+    inner_q = inner[:, :rank].astype(bf16)
+    inner_k = inner[:, rank : 2 * rank].astype(bf16)
     inner_v = inner[:, 2 * rank :].astype(bf16)
 
-    q_od = vf_b[:, :q_rows, :].reshape(reps * q_rows, 2 * rank)
-    kv_up = (
-        vf_b[:, q_rows + up_rows :, :]
-        .astype(f32)
-        .reshape(reps * kv_rows, 2 * rank)
-        .astype(bf16)
-    )
-    q = q_acc[...] + adapter_scale * nt_dot(inner_q, q_od)
-    nk = kv_acc[0] + adapter_scale * nt_dot(inner_k, kv_up)
-    nv = kv_acc[1] + adapter_scale * nt_dot(inner_v, kv_up[:, :rank])
-
-    cosv, sinv = cos[...], sin[...]
+    def rows_of(j):
+        w = g_kv.shape[2]
+        return g_kv[:, j].astype(f32).reshape(reps * w, rank).astype(bf16)
+
+    q_up = jnp.concatenate([g_q[s] for s in range(reps)], axis=1)
+    q = q_acc[...] + adapter_scale * nn_dot(inner_q, q_up)
+    nk = kv_acc[0] + adapter_scale * nt_dot(inner_k, rows_of(0))
+    nv = kv_acc[1] + adapter_scale * nt_dot(inner_v, rows_of(1))
+
+    across(2)
+    across(3)
+
+    cosv = jnp.cos(angle[...])
+    sinv = jnp.sin(angle[...])
+    lane = lax.broadcasted_iota(jnp.int32, (seqs, head_dim), 1)
+    sinv = jnp.where(lane < half_dim, -sinv, sinv)
 
     def turn(x):
         return x * cosv + pltpu.roll(x, head_dim // 2, 1) * sinv
@@ -360,7 +398,7 @@
     cache = cache_k.shape[2]
     span = kv_local * cache
     score_scale = 1.0 / math.sqrt(head_dim)
-    bs = 8
+    bs = min(16, ps)
     per = ps // bs
 
     @pl.loop(0, seqs // bs)
@@ -382,6 +420,7 @@
         col_id = lax.broadcasted_iota(jnp.int32, (pad_heads, span), 1)
         mine = jnp.minimum(row_id // group, kv_local - 1) == col_id // cache
         pos = lax.rem(col_id, cache)
+        scored = []
         for b in range(bs):
             sl = slice(b * pad_heads, (b + 1) * pad_heads)
             stack = jnp.concatenate([hi[sl], mid[sl], low[sl]], axis=0).astype(bf16)
@@ -393,24 +432,29 @@
                 + dots[2 * pad_heads :]
             ) * score_scale
             live = jnp.logical_and(mine, pos < lengths[i * bs + b])
-            top = jnp.maximum(
-                jnp.max(jnp.where(live, sc, -1e30), axis=-1, keepdims=True), own[sl]
-            )
-            w = jnp.where(live, jnp.exp(sc - top), 0.0)
-            ow = jnp.exp(own[sl] - top)
-            denom = jnp.sum(w, axis=-1, keepdims=True) + ow
-            probs = (w / denom).astype(bf16)
-            own_p = (ow / denom).astype(bf16).astype(f32)
+            scored.append(jnp.where(live, sc, -1e30))
+        sc = jnp.concatenate(scored, axis=0)
+        top = jnp.maximum(jnp.max(sc, axis=-1, keepdims=True), own)
+        w = jnp.exp(sc - top)
+        ow = jnp.exp(own - top)
+        scale = 1.0 / (jnp.sum(w, axis=-1, keepdims=True) + ow)
+        probs = w * scale
+        own_part = (ow * scale).astype(bf16).astype(f32) * nv3[rows, :]
+        for b in range(bs):
+            sl = slice(b * pad_heads, (b + 1) * pad_heads)
             vals = v_b[i * bs + b].reshape(span, head_dim)
             here = pl.ds(base + b * pad_heads, pad_heads)
-            c3[here, :] = nn_dot(probs, vals) + own_p * nv3[here, :]
+            c3[here, :] = nn_dot(probs[sl].astype(bf16), vals) + own_part[sl]
 
     for h in range(heads):
         ctx[:, h * head_dim : (h + 1) * head_dim] = c3[
             pl.ds(h, seqs, stride=pad_heads), :
         ].astype(bf16)
 
-    mid_s[...] = nn_dot(ctx[...], q_od)
+    settled(2)
+    settled(3)
+    down_t = jnp.concatenate([g_od[s] for s in range(reps)], axis=1)
+    mid_s[...] = nt_dot(ctx[...], down_t)
     mid_sends = []
     for j in range(1, n):
         c = remote(mid_s, mid_r.at[j], mid_ssem.at[j], mid_rsem.at[j], r, lax.rem(t + j, n))
@@ -449,24 +493,19 @@
         c.start()
         rs_sends.append((c, k))
 
-    total_mid = mid_s[:, rank:]
+    total_mid = mid_s[...]
     for c in mid_sends:
         c.wait_recv()
     for j in range(1, n):
-        total_mid = total_mid + mid_r[j][:, rank:]
+        total_mid = total_mid + mid_r[j]
     middle = total_mid.astype(bf16)
-    ups = vf_b[:, q_rows : q_rows + up_rows, :].astype(f32)
-    up_full = (
-        jnp.concatenate([ups[:, :, :rank], ups[:, :, rank:]], axis=1)
-        .reshape(reps * 2 * up_rows, rank)
-        .astype(bf16)
-    )
+    up_full = jnp.concatenate([g_ou[s] for s in range(reps)], axis=1)
     final = []
     for half in range(2):
         wo_copy(0, half).wait()
         final.append(
             nn_dot(ctx[...], wo_b[half])
-            + adapter_scale * nt_dot(middle, up_full[half * half_w : (half + 1) * half_w])
+            + adapter_scale * nn_dot(middle, up_full[:, half * half_w : (half + 1) * half_w])
         )
     for c, k in rs_sends:
         if k == 1:
@@ -478,15 +517,8 @@
                 value = value + rs_r[offsets[ci]].astype(f32)
         out[:, half * half_w : (half + 1) * half_w] = value.astype(bf16)
 
-    for c in dn_sends + dn_fwd + v_fwd + in_sends + mid_sends:
+    for c in dn_sends + dn_fwd + a_sends + g_sends + in_sends + mid_sends:
         c.wait_send()
-    for j in range(1, half_reps):
-        v_sends[j].wait_send()
-
-    @pl.when(plane != t)
-    def _():
-        v_sends[0].wait_send()
-
     for c, _k in rs_sends:
         c.wait_send()
 
@@ -522,28 +554,13 @@
         down = lax.dynamic_update_slice(
             jnp.zeros((3 * rank, win), down.dtype), down, (0, spot)
         )
-    q_rows = query_up_factor.shape[1]
-    kv_rows = key_value_up_factors.shape[2]
-    up = output_up_factor.T
-    up_rows = up.shape[0] // 2
-    packed = jnp.concatenate(
-        [
-            jnp.concatenate([query_up_factor.T, output_down_factor], axis=1),
-            jnp.concatenate([up[:up_rows], up[up_rows:]], axis=1),
-            jnp.concatenate([key_value_up_factors[1].T, key_value_up_factors[0].T], axis=1),
-        ],
-        axis=0,
-    )
-    half_dim = head_dim // 2
-    frequency = rope_base ** (-(jnp.arange(half_dim, dtype=f32) * 2.0) / head_dim)
-    angles = lengths.astype(f32)[:, None] * frequency[None, :]
-    cosine, sine = jnp.cos(angles), jnp.sin(angles)
-    cos2 = jnp.concatenate([cosine, cosine], axis=1)
-    sin2 = jnp.concatenate([-sine, sine], axis=1)
-
+    f_q = query_up_factor
+    f_kv = jnp.swapaxes(key_value_up_factors, 1, 2)
+    f_od = output_down_factor.T
+    f_ou = output_up_factor
+    factors = (f_q, f_kv, f_od, f_ou)
     dims = dict(
         tp=n, rep=reps, rank=rank, block=block, win=win,
-        q_rows=q_rows, up_rows=up_rows, kv_rows=kv_rows,
     )
     pad_heads = -(-heads // 8) * 8
     wide = depth // n
@@ -560,7 +577,7 @@
         functools.partial(kernel, dims),
         name="decode_block",
         out_shape=jax.ShapeDtypeStruct((seqs, wide), bf16),
-        in_specs=[hbm, vmem, hbm, hbm, hbm, hbm, hbm, hbm, hbm, smem, vmem, vmem],
+        in_specs=[hbm, vmem] + [hbm] * 10 + [smem],
         out_specs=vmem,
         scratch_shapes=[
             vec((seqs, depth), bf16),
@@ -571,8 +588,9 @@
             vec((seqs, kv_local, cache, head_dim), bf16),
             vec((seqs, kv_local, cache, head_dim), bf16),
             vec((reps, 3 * rank, win), bf16),
-            vec(packed.shape, bf16),
-            vec((reps,) + packed.shape, bf16),
+            *[vec((reps // 2,) + f.shape, bf16) for f in factors],
+            *[vec((reps,) + f.shape, bf16) for f in factors],
+            vec((seqs, head_dim), f32),
             vec((seqs, width), f32),
             vec((2, seqs, kv_local * head_dim), f32),
             vec((seqs, 3 * rank), f32),
@@ -582,8 +600,8 @@
             vec((rows, head_dim), f32),
             vec((rows, head_dim), f32),
             vec((seqs, width), bf16),
-            vec((seqs, 2 * rank), f32),
-            vec((n, seqs, 2 * rank), f32),
+            vec((seqs, rank), f32),
+            vec((n, seqs, rank), f32),
             vec((slots, seqs, half_w), bf16),
             vec((slots, seqs, half_w), bf16),
             dma,
@@ -592,13 +610,15 @@
             dma((2 * n,)),
             dma((parts,)),
             dma((parts,)),
-            dma((2,)),
+            dma((1 + len(factors),)),
             dma((reps // 2,)),
             dma((reps,)),
             dma((reps // 2,)),
-            dma((reps // 2,)),
-            dma((reps,)),
-            dma((reps // 2,)),
+            dma((len(factors), reps // 2)),
+            dma((len(factors), reps // 2)),
+            dma((len(factors), reps)),
+            dma((len(factors), reps)),
+            dma((len(factors), reps)),
             dma((n,)),
             dma((n,)),
             dma((n,)),
@@ -616,12 +636,10 @@
         key_value_weight,
         output_weight_matrix,
         down,
-        packed,
+        *factors,
         cache_keys,
         cache_values,
         lengths,
-        cos2,
-        sin2,
     )
 
 

time: 84 us -> 59.3 us (0.71)
  Pallas kernels: 74.9 us -> 56 us
  local copies, waits for them, and re-layouts: 6.28 us -> 3.02 us
  other arithmetic: 2.3 us -> 0 us
    pallas_call x1, Pallas kernels: 74.9 us -> 56 us  [local(): pl.pallas_call(functools.partial(kernel, dims), name='decode_block', out_...]
    unnamed x4 -> x1, local copies, waits for them, and re-layouts: 4.21 us -> 1.67 us
    concatenate x2 -> x0, other arithmetic: 1.44 us -> none  [the longest x1 0.73 us: local(): jnp.concatenate([jnp.concatenate([query_up_factor.T, output_down_factor],...]
where the time goes in v2:
time: 59.3 us; the launch traced here: 59 us
  Pallas kernels  56 us (94%)
  local copies, waits for them, and re-layouts  3.02 us (5%)
    pallas_call x1, Pallas kernels, local(): pl.pallas_call(functools.partial(kernel, dims), name='decode_block', out_...  56 us
    unnamed x1, local copies, waits for them, and re-layouts  1.67 us
    reshape x1, local copies, waits for them, and re-layouts, local(): norm_gain.reshape(1, -1)  1.35 us

profile of v2, /device:TPU:0, one launch (start us, length us, event | category | flops | bytes accessed | tf_op | source)
XLA Modules:
  0.0 59.0 jit_solution(17170411243647075696)
XLA Ops:
  0.0 1.3 %reshape.6.gain = bf16[1,8192]{1,0:T(2,128)(2,1)} reshape(bf16[8192]{0:T(1024)(128)(2,1)} %param.14) | data formatting | bytes 32768 | tf_op jit(solution)/shard_map/reshape | solution.py:634
  1.4 56.0 %decode_block.1 = bf16[64,2048]{1,0:T(8,128)(2,1)} custom-call(bf16[64,8192]{1,0:T(8,128)(2,1)} %hidden.1, bf16[1,8192]{1,0:T(2,128)(2,1)} %reshape.6.gain, bf16[8192,1024]{1,0:T(8,128)(2,1)} %wq.1, bf16[2,8192,256]{2,1,0:T(8,128)(2,1)} %wkv.1, bf16[1024,8192]{1,0:T(8,128)(2,1)} %wo.1, bf16[192,256]{1,0:T(8,128)(2,1)} %bitcast.5, bf16[64,128]{1,0:T(8,128)(2,1)} %f_q.1, ...), custom_call_target="tpu_custom_call" | custom-call | tf_op jit(solution)/shard_map/decode_block/pallas_call | solution.py:576
  57.4 1.7 %copy.15 = bf16[64,2048]{1,0:T(8,128)(2,1)} copy(bf16[64,2048]{1,0:T(8,128)(2,1)} %decode_block.1) | data formatting | bytes 524288

commit v3 on v2

--- a/solution.py
+++ b/solution.py
@@ -67,6 +67,7 @@
     angle,
     q_acc,
     kv_acc,
+    inner_o,
     inner_s,
     inner_r,
     q3,
@@ -223,7 +224,9 @@
     for c in dn_sends:
         c.start()
     a_sends = []
-    for f, buf in enumerate(spread):
+
+    def to_chips(f):
+        buf = spread[f]
         own_f[f].wait()
         for j in range(1, half_reps):
             c = remote(
@@ -233,6 +236,8 @@
             c.start()
             a_sends.append(c)
 
+    to_chips(0)
+    to_chips(1)
     per_plane = reps // n
     groups = per_plane // 2
     g_sends = []
@@ -333,7 +338,8 @@
         start = (j * n + t) * block
         cols = pl.ds(pl.multiple_of(start // win * win, LANES), win)
         part = part + nt_dot(norm_b[:, cols], dn_b[j])
-    inner_s[...] = part
+    inner_s[...] = part.astype(bf16)
+    inner_o[...] = part
     in_sends = []
     for j in range(1, n):
         c = remote(
@@ -344,17 +350,20 @@
 
     across(0)
     across(1)
+    to_chips(2)
+    to_chips(3)
+    project(steps // 2, 3 * steps // 4)
     to_planes(2)
     to_planes(3)
-    project(steps // 2, steps)
+    project(3 * steps // 4, steps)
     settled(0)
     settled(1)
 
-    total = inner_s[...]
+    total = inner_o[...]
     for c in in_sends:
         c.wait_recv()
     for j in range(1, n):
-        total = total + inner_r[j]
+        total = total + inner_r[j].astype(f32)
     inner = total.astype(bf16).astype(f32)
     inner_q = inner[:, :rank].astype(bf16)
     inner_k = inner[:, rank : 2 * rank].astype(bf16)
@@ -401,8 +410,7 @@
     bs = min(16, ps)
     per = ps // bs
 
-    @pl.loop(0, seqs // bs)
-    def _(i):
+    def attend(i):
         @pl.when(lax.rem(i, per) == 0)
         def _():
             for c in cache_copies(i // per):
@@ -446,20 +454,15 @@
             here = pl.ds(base + b * pad_heads, pad_heads)
             c3[here, :] = nn_dot(probs[sl].astype(bf16), vals) + own_part[sl]
 
-    for h in range(heads):
-        ctx[:, h * head_dim : (h + 1) * head_dim] = c3[
-            pl.ds(h, seqs, stride=pad_heads), :
-        ].astype(bf16)
-
-    settled(2)
-    settled(3)
-    down_t = jnp.concatenate([g_od[s] for s in range(reps)], axis=1)
-    mid_s[...] = nt_dot(ctx[...], down_t)
-    mid_sends = []
-    for j in range(1, n):
-        c = remote(mid_s, mid_r.at[j], mid_ssem.at[j], mid_rsem.at[j], r, lax.rem(t + j, n))
-        c.start()
-        mid_sends.append(c)
+    waves = rs_s.shape[0]
+    ws = seqs // waves
+
+    def attend_wave(wave):
+        pl.loop(wave * ws // bs, (wave + 1) * ws // bs)(attend)
+        for h in range(heads):
+            ctx[wave * ws : (wave + 1) * ws, h * head_dim : (h + 1) * head_dim] = c3[
+                pl.ds(wave * ws * pad_heads + h, ws, stride=pad_heads), :
+            ].astype(bf16)
 
     tile = min(512, half_w)
     offsets = []
@@ -468,36 +471,65 @@
         offsets.append(at)
         at += hops
     rs_sends = []
-    for ci, way, half, hops, k in sends:
+
+    def hop(wave, place, way):
+        return remote(
+            rs_s.at[wave, place], rs_r.at[wave, place], rs_ssem.at[wave, place],
+            rs_rsem.at[wave, place], r, lax.rem(t + way + n, n),
+        )
+
+    def pass_on(wave, ci, way, half, hops, k):
         idx = ((way * k) % n) * 2 + half
-        wo_copy(way * k, half).wait()
         place = offsets[ci] + k - 1
+        if wave == 0:
+            wo_copy(way * k, half).wait()
         if k < hops:
-            remote(
-                rs_s.at[place + 1], rs_r.at[place + 1], rs_ssem.at[place + 1],
-                rs_rsem.at[place + 1], r, lax.rem(t + way + n, n),
-            ).wait_recv()
+            hop(wave, place + 1, way).wait_recv()
 
         @pl.loop(0, half_w // tile)
         def _(i):
             cols = pl.ds(pl.multiple_of(i * tile, tile), tile)
-            value = nn_dot(ctx[...], wo_b[idx, :, cols])
+            value = nn_dot(ctx[wave * ws : (wave + 1) * ws, :], wo_b[idx, :, cols])
             if k < hops:
-                value = value + rs_r[place + 1, :, cols].astype(f32)
-            rs_s[place, :, cols] = value.astype(bf16)
-
-        c = remote(
-            rs_s.at[place], rs_r.at[place], rs_ssem.at[place], rs_rsem.at[place],
-            r, lax.rem(t + way + n, n),
-        )
+                value = value + rs_r[wave, place + 1, :, cols].astype(f32)
+            rs_s[wave, place, :, cols] = value.astype(bf16)
+
+        c = hop(wave, place, way)
         c.start()
         rs_sends.append((c, k))
 
-    total_mid = mid_s[...]
+    early = [x for x in sends if x[3] == x[4] == n // 2]
+    lone = [x for x in sends if x[3] == x[4] != n // 2]
+    joined = [x for x in sends if x[3] != x[4]]
+    attend_wave(0)
+    for x in early + lone:
+        pass_on(0, *x)
+    for wave in range(1, waves):
+        attend_wave(wave)
+        for x in early:
+            pass_on(wave, *x)
+        for x in joined:
+            pass_on(wave - 1, *x)
+        for x in lone:
+            pass_on(wave, *x)
+
+    settled(2)
+    settled(3)
+    down_t = jnp.concatenate([g_od[s] for s in range(reps)], axis=1)
+    total_mid = nt_dot(ctx[...], down_t)
+    mid_s[...] = total_mid.astype(bf16)
+    mid_sends = []
+    for j in range(1, n):
+        c = remote(mid_s, mid_r.at[j], mid_ssem.at[j], mid_rsem.at[j], r, lax.rem(t + j, n))
+        c.start()
+        mid_sends.append(c)
+    for x in joined:
+        pass_on(waves - 1, *x)
+
     for c in mid_sends:
         c.wait_recv()
     for j in range(1, n):
-        total_mid = total_mid + mid_r[j]
+        total_mid = total_mid + mid_r[j].astype(f32)
     middle = total_mid.astype(bf16)
     up_full = jnp.concatenate([g_ou[s] for s in range(reps)], axis=1)
     final = []
@@ -514,7 +546,7 @@
         value = final[half]
         for ci, (_way, h2, hops) in enumerate(channels_of(n)):
             if h2 == half and hops > 0:
-                value = value + rs_r[offsets[ci]].astype(f32)
+                value = value + rs_r[:, offsets[ci]].reshape(seqs, half_w).astype(f32)
         out[:, half * half_w : (half + 1) * half_w] = value.astype(bf16)
 
     for c in dn_sends + dn_fwd + a_sends + g_sends + in_sends + mid_sends:
@@ -567,7 +599,7 @@
     half_w = wide // 2
     rows = seqs * pad_heads
     slots = sum(hops for _, _, hops in channels_of(n))
-    steps, parts = 16, 4
+    steps, parts, waves = 16, 4, 2
     dma = pltpu.SemaphoreType.DMA
     hbm = pl.BlockSpec(memory_space=pl.ANY)
     vmem = pl.BlockSpec(memory_space=pltpu.VMEM)
@@ -594,16 +626,17 @@
             vec((seqs, width), f32),
             vec((2, seqs, kv_local * head_dim), f32),
             vec((seqs, 3 * rank), f32),
-            vec((n, seqs, 3 * rank), f32),
+            vec((seqs, 3 * rank), bf16),
+            vec((n, seqs, 3 * rank), bf16),
             vec((rows, head_dim), f32),
             vec((rows, head_dim), f32),
             vec((rows, head_dim), f32),
             vec((rows, head_dim), f32),
             vec((seqs, width), bf16),
-            vec((seqs, rank), f32),
-            vec((n, seqs, rank), f32),
-            vec((slots, seqs, half_w), bf16),
-            vec((slots, seqs, half_w), bf16),
+            vec((seqs, rank), bf16),
+            vec((n, seqs, rank), bf16),
+            vec((waves, slots, seqs // waves, half_w), bf16),
+            vec((waves, slots, seqs // waves, half_w), bf16),
             dma,
             dma((steps,)),
             dma((steps,)),
@@ -623,8 +656,8 @@
             dma((n,)),
             dma((n,)),
             dma((n,)),
-            dma((slots,)),
-            dma((slots,)),
+            dma((waves, slots)),
+            dma((waves, slots)),
         ],
         compiler_params=pltpu.CompilerParams(
             collective_id=0, has_side_effects=True, vmem_limit_bytes=66000000

time: 59.3 us -> 54.4 us (0.917)
  Pallas kernels: 56 us -> 51.1 us
    pallas_call x1, Pallas kernels: 56 us -> 51.1 us  [local(): pl.pallas_call(functools.partial(kernel, dims), name='decode_block', out_...]
where the time goes in v3:
time: 54.4 us; the launch traced here: 54.1 us
  Pallas kernels  51.1 us (94%)
  local copies, waits for them, and re-layouts  3.02 us (6%)
    pallas_call x1, Pallas kernels, local(): pl.pallas_call(functools.partial(kernel, dims), name='decode_block', out_...  51.1 us
    unnamed x1, local copies, waits for them, and re-layouts  1.67 us
    reshape x1, local copies, waits for them, and re-layouts, local(): norm_gain.reshape(1, -1)  1.35 us

profile of v3, /device:TPU:0, one launch (start us, length us, event | category | flops | bytes accessed | tf_op | source)
XLA Modules:
  0.0 54.1 jit_solution(12476674408030576051)
XLA Ops:
  0.0 1.3 %reshape.6.gain = bf16[1,8192]{1,0:T(2,128)(2,1)} reshape(bf16[8192]{0:T(1024)(128)(2,1)} %param.14) | data formatting | bytes 32768 | tf_op jit(solution)/shard_map/reshape | solution.py:667
  1.4 51.1 %decode_block.1 = bf16[64,2048]{1,0:T(8,128)(2,1)} custom-call(bf16[64,8192]{1,0:T(8,128)(2,1)} %hidden.1, bf16[1,8192]{1,0:T(2,128)(2,1)} %reshape.6.gain, bf16[8192,1024]{1,0:T(8,128)(2,1)} %wq.1, bf16[2,8192,256]{2,1,0:T(8,128)(2,1)} %wkv.1, bf16[1024,8192]{1,0:T(8,128)(2,1)} %wo.1, bf16[192,256]{1,0:T(8,128)(2,1)} %bitcast.5, bf16[64,128]{1,0:T(8,128)(2,1)} %f_q.1, ...), custom_call_target="tpu_custom_call" | custom-call | tf_op jit(solution)/shard_map/decode_block/pallas_call | solution.py:608
  52.5 1.7 %copy.15 = bf16[64,2048]{1,0:T(8,128)(2,1)} copy(bf16[64,2048]{1,0:T(8,128)(2,1)} %decode_block.1) | data formatting | bytes 524288

commit v4 on v3

--- a/solution.py
+++ b/solution.py
@@ -300,7 +300,7 @@
         x = hid_b[rows, :].astype(f32)
         square = jnp.mean(x * x, axis=-1, keepdims=True)
         norm_b[rows, :] = (
-            x * lax.rsqrt(square + epsilon) * gain[...].astype(f32)
+            x * lax.rsqrt(square + epsilon) * gain[...].astype(f32).reshape(1, depth)
         ).astype(bf16)
 
     q_acc[...] = jnp.zeros_like(q_acc)
@@ -318,10 +318,6 @@
                 kv_acc[j] += nn_dot(x, wkv_b[j, rows, :])
 
     project(0, steps // 4)
-    to_planes(0)
-    to_planes(1)
-    project(steps // 4, steps // 2)
-
     dn_fwd = []
     for j in range(half_reps - 1, 0, -1):
         src = lax.rem(r + 2 * j, reps)
@@ -329,6 +325,10 @@
         c = remote(dn_b.at[src], dn_b.at[src], dn_fsem.at[j], dn_rsem.at[src], partner, t)
         c.start()
         dn_fwd.append(c)
+    to_planes(0)
+    to_planes(1)
+    project(steps // 4, steps // 2)
+
     for j in range(half_reps):
         src = lax.rem(partner + 2 * j, reps)
         remote(dn_b.at[src], dn_b.at[src], dn_fsem.at[j], dn_rsem.at[src], partner, t).wait_recv()
@@ -664,7 +664,7 @@
         ),
     )(
         hidden,
-        norm_gain.reshape(1, -1),
+        norm_gain,
         query_weight_matrix,
         key_value_weight,
         output_weight_matrix,

time: 54.4 us -> 51.7 us (0.950)
  local copies, waits for them, and re-layouts: 3.02 us -> 1.67 us
  Pallas kernels: 51.1 us -> 49.8 us
    reshape x1 -> x0, local copies, waits for them, and re-layouts: 1.35 us -> none  [local(): norm_gain.reshape(1, -1)]
    pallas_call x1, Pallas kernels: 51.1 us -> 49.8 us  [local(): pl.pallas_call(functools.partial(kernel, dims), name='decode_block', out_...]
where the time goes in v4:
time: 51.7 us; the launch traced here: 51.5 us
  Pallas kernels  49.8 us (96%)
  local copies, waits for them, and re-layouts  1.67 us (3%)
    pallas_call x1, Pallas kernels, local(): pl.pallas_call(functools.partial(kernel, dims), name='decode_block', out_...  49.8 us
    unnamed x1, local copies, waits for them, and re-layouts  1.67 us

profile of v4, /device:TPU:0, one launch (start us, length us, event | category | flops | bytes accessed | tf_op | source)
XLA Modules:
  0.0 51.5 jit_solution(13229325851704873348)
XLA Ops:
  0.0 49.8 %decode_block.1 = bf16[64,2048]{1,0:T(8,128)(2,1)} custom-call(bf16[64,8192]{1,0:T(8,128)(2,1)} %hidden.1, bf16[8192]{0:T(1024)(128)(2,1)} %gain.1, bf16[8192,1024]{1,0:T(8,128)(2,1)} %wq.1, bf16[2,8192,256]{2,1,0:T(8,128)(2,1)} %wkv.1, bf16[1024,8192]{1,0:T(8,128)(2,1)} %wo.1, bf16[192,256]{1,0:T(8,128)(2,1)} %bitcast.5, bf16[64,128]{1,0:T(8,128)(2,1)} %f_q.1, ...), custom_call_target="tpu_custom_call" | custom-call | tf_op jit(solution)/shard_map/decode_block/pallas_call | solution.py:608
  49.8 1.7 %copy.15 = bf16[64,2048]{1,0:T(8,128)(2,1)} copy(bf16[64,2048]{1,0:T(8,128)(2,1)} %decode_block.1) | data formatting | bytes 524288
